TPU v7x, 32 devices: a whole 2x2x4 slice. The times are simulated.
32 devices in a mesh: site: 2 (over y), pts: 16 (over z, x, core).
Axes of the slice: x: 2, y: 2, z: 4, core: 2. Of those that a mesh axis runs over, the one named last changes fastest.
Arguments:
- green_tensors: bfloat16 [512, 4, 6, 2, 1024], P(('site', 'pts')), parts along dimension 0, may hold values from -6 to 6
- block_lists: int32 [32, 32], P(('site', 'pts')), parts along dimension 0, may hold values from 0 to 255, as said below
- block_count: int32 [32], P(('site', 'pts')), parts along dimension 0, may hold values from 1 to 32
- onset_steps: int32 [32, 16, 128], P(('site', 'pts')), parts along dimension 0, may hold values from 0 to 255
- slip_amount: float32 [32, 16, 128], P(('site', 'pts')), parts along dimension 0, may hold values from 0.2 to 2
- mechanism: float32 [32, 6], P(('site', 'pts')), parts along dimension 0, may hold values from -2.4 to 2.4
- slip_rate: float32 [32, 16, 128], P(('site', 'pts')), parts along dimension 0, may hold values from 0.005 to 0.05
Outputs:
- seismograms: float32 [32, 16, 2, 1024], P(('site', 'pts')), parts along dimension 0
There are 2 independent parts, one for each index of `site`. A program takes and returns all parts, laid end to end along the dimension named above; each array names one. Nothing has to cross between parts.
Inputs may be any that keep to these rules, and one draw needn't show every extreme that they name: `block_lists`: numbers of point blocks; the ruptures held by one device name at most 2 entries in blocks held by any one device, and exactly 2 for some holder.
All inputs are finite; a program needn't handle non-finite values.
Results may differ from a plain program's by a relative error of at most 0.0003.
Values may be sent and summed in bfloat16 or wider, within the bound.
A program may use at most 128 MiB of HBM per device.

v0:
```python
import functools

import jax
import jax.numpy as jnp
from jax import lax
from jax.experimental import pallas as pl
from jax.experimental.pallas import tpu as pltpu
from jax.sharding import PartitionSpec as P

LANES = 128


def seismogram_kernel(n, cap, points, comps, width, listed, wants_s_ref, mech_s_ref, count_ref,
                      wants_ref, green_ref, onset_ref, slip_ref, rate_ref, out_ref,
                      wanted, mech, mechs, wanted_s, outbox, out_scale, inbox, in_scale,
                      motion, high_taps, low_taps, onset_of, slip_of,
                      send_w, recv_w, send_m, recv_m, local_sem, send_t, recv_t, send_s, recv_s):
    me = lax.axis_index("pts")
    rows = points * comps
    length = out_ref.shape[-1]
    tiles = length // LANES
    half = tiles // 2
    strains = width // rows
    variations = onset_ref.shape[0]
    mesh_id = pl.DeviceIdType.MESH
    lane = lax.broadcasted_iota(jnp.int32, (8, LANES), 1)
    sub = lax.broadcasted_iota(jnp.int32, (8, LANES), 0)

    barrier = pltpu.get_barrier_semaphore()

    def greet(d, carry):
        pl.semaphore_signal(barrier, inc=1, device_id={"pts": lax.rem(me + d, n)},
                            device_id_type=mesh_id)
        return carry

    lax.fori_loop(1, n, greet, 0)

    out_row = lax.broadcasted_iota(jnp.int32, (rows, LANES), 0)
    in_row = lax.broadcasted_iota(jnp.int32, (rows, LANES), 1)
    table = jnp.zeros((rows, LANES), jnp.float32)
    for p in range(points):
        for s in range(strains):
            for c in range(comps):
                here = (out_row == p * comps + c) & (in_row == (p * strains + s) * comps + c)
                table = jnp.where(here, mech_s_ref[0, s], table)
    mech[...] = table
    mechs[0] = table
    wanted[0] = wants_ref[me]
    pl.semaphore_wait(barrier, n - 1)

    def remote(src, dst, send, recv, d):
        return pltpu.make_async_remote_copy(
            src_ref=src, dst_ref=dst.at[n - d], send_sem=send.at[d], recv_sem=recv.at[n - d],
            device_id={"pts": lax.rem(me + d, n)}, device_id_type=mesh_id)

    def want_copy(d):
        return remote(wants_ref.at[lax.rem(me + d, n)], wanted, send_w, recv_w, d)

    def mech_copy(d):
        return remote(mech, mechs, send_m, recv_m, d)

    def trace_copy(d):
        return remote(outbox.at[d], inbox, send_t, recv_t, d)

    def scale_copy(d):
        return remote(out_scale.at[d], in_scale, send_s, recv_s, d)

    def start_meta(d, carry):
        want_copy(d).start()
        mech_copy(d).start()
        return carry

    lax.fori_loop(1, n, start_meta, 0)

    i_row = lax.broadcasted_iota(jnp.int32, (LANES, LANES), 0)
    j_lane = lax.broadcasted_iota(jnp.int32, (LANES, LANES), 1)
    near_mask = j_lane >= i_row
    motion[...] = jnp.zeros(motion.shape, jnp.float32)

    for v in range(variations):
        rate = jnp.broadcast_to(rate_ref[v:v + 1, :], (LANES, LANES))
        turned = pltpu.roll(rate, 0, 1, stride=1, stride_axis=0)
        both = jnp.concatenate(
            [jnp.where(near_mask, turned, 0.0), jnp.where(near_mask, 0.0, turned)], axis=0)
        high = both.astype(jnp.bfloat16)
        high_taps[v] = high
        low_taps[v] = (both - high.astype(jnp.float32)).astype(jnp.bfloat16)

    def spread(q, carry):
        pick = jnp.full((variations, LANES), q, jnp.int32)
        onset_of[q] = jnp.take_along_axis(onset_ref[...], pick, axis=1)
        slip_of[q] = jnp.take_along_axis(slip_ref[...], pick, axis=1)
        return carry

    lax.fori_loop(0, listed * points, spread, 0, unroll=4)

    def wait_meta(d, carry):
        want_copy(d).wait()
        mech_copy(d).wait()
        return carry

    lax.fori_loop(1, n, wait_meta, 0)
    to_scalar = pltpu.make_async_copy(wanted, wanted_s, local_sem)
    to_scalar.start()
    to_scalar.wait()

    def encode(d, box, scale_box, at):
        lhs = mechs[d][:, :width]
        high = lhs.astype(jnp.bfloat16).astype(jnp.float32)
        rest = lhs - high
        mid = rest.astype(jnp.bfloat16).astype(jnp.float32)
        stack = jnp.concatenate([high, mid, rest - mid], axis=0).astype(jnp.bfloat16)
        scales = jnp.zeros((8, LANES), jnp.float32)
        for slot in range(cap):
            block = green_ref[wanted_s[d, 0, slot]]
            parts = jnp.dot(stack, block, preferred_element_type=jnp.float32)
            full = parts[0:rows] + (parts[rows:2 * rows] + parts[2 * rows:3 * rows])
            cut = [full[:, i * LANES:(i + 1) * LANES] for i in range(tiles)]
            top = jnp.abs(cut[0])
            for part in cut[1:]:
                top = jnp.maximum(top, jnp.abs(part))
            top = jnp.max(top, axis=1, keepdims=True)
            inverse = 32767.0 / jnp.maximum(top, 1e-30)
            coded = [jnp.floor(part * inverse + 0.5).astype(jnp.int32) for part in cut]
            scales = jnp.where(lane == slot * rows + sub, top * (1.0 / 32767.0), scales)
            for i in range(half):
                word = jnp.bitwise_or(jnp.left_shift(coded[i + half], 16),
                                      jnp.bitwise_and(coded[i], 0xFFFF))
                box[at, slot, :, i * LANES:(i + 1) * LANES] = word
        scale_box[at] = jnp.sum(scales, axis=0, keepdims=True)

    def send(d, carry):
        encode(d, outbox, out_scale, d)

        @pl.when(d > 1)
        def _():
            trace_copy(d - 1).start()
            scale_copy(d - 1).start()

        return carry

    lax.fori_loop(1, n, send, 0)
    encode(0, inbox, in_scale, 0)
    trace_copy(n - 1).start()
    scale_copy(n - 1).start()

    def arrive(step, carry):
        j = lax.rem(n - step, n)
        source_device = lax.rem(me + j, n)

        @pl.when(step > 0)
        def _():
            trace_copy(step).wait_recv()
            scale_copy(step).wait_recv()

        scales = jnp.broadcast_to(in_scale[j], (8, LANES))
        scale_of = [jnp.take_along_axis(scales, jnp.full((8, LANES), q, jnp.int32), axis=1)
                    for q in range(cap * rows)]
        for group in range(variations // 8):
            acc = [motion[comps + q, group * 8:group * 8 + 8, :] for q in range(tiles * comps)]
            for slot in range(cap):
                k = wants_s_ref[source_device, 0, cap + slot]
                used = jnp.where(jnp.full((8, LANES), k, jnp.int32) < count_ref[0], 1.0, 0.0)
                base = jnp.minimum(k, listed - 1) * points
                for p in range(points):
                    onset = onset_of[base + p, group * 8:group * 8 + 8, :]
                    slip = slip_of[base + p, group * 8:group * 8 + 8, :] * used
                    shift = jnp.bitwise_and(onset, LANES - 1)
                    back = jnp.right_shift(onset, 7) + (lane >= LANES - shift).astype(jnp.int32)
                    one = back >= 1
                    two = back >= 2
                    source = jnp.bitwise_and(lane - shift, LANES - 1)
                    for c in range(comps):
                        row = p * comps + c
                        weight = slip * scale_of[slot * rows + row]
                        words = [jnp.broadcast_to(
                            inbox[j, slot, row:row + 1, i * LANES:(i + 1) * LANES], (8, LANES))
                            for i in range(half)]
                        prev2 = jnp.left_shift(words[half - 2], 16)
                        prev1 = jnp.left_shift(words[half - 1], 16)
                        for i in range(half):
                            cur = words[i]
                            mixed = jnp.where(two, prev2, jnp.where(one, prev1, cur))
                            moved = jnp.take_along_axis(mixed, source, axis=1)
                            low = jnp.right_shift(jnp.left_shift(moved, 16), 16)
                            high = jnp.right_shift(moved, 16)
                            acc[i * comps + c] += weight * low.astype(jnp.float32)
                            acc[(i + half) * comps + c] += weight * high.astype(jnp.float32)
                            prev2, prev1 = prev1, cur
            for q in range(tiles * comps):
                motion[comps + q, group * 8:group * 8 + 8, :] = acc[q]
        return carry

    lax.fori_loop(0, n, arrive, 0)

    count = tiles * comps
    for v in range(variations):
        lhs = jnp.concatenate([motion[comps:comps + count, v, :], motion[0:count, v, :]], axis=1)
        high = lhs.astype(jnp.bfloat16).astype(jnp.float32)
        pair = jnp.concatenate([high, lhs - high], axis=0).astype(jnp.bfloat16)
        main = jnp.dot(pair, high_taps[v], preferred_element_type=jnp.float32)
        minor = jnp.dot(pair[:count], low_taps[v], preferred_element_type=jnp.float32)
        result = main[:count] + (main[count:] + minor)
        for i in range(tiles):
            out_ref[v, :, i * LANES:(i + 1) * LANES] = result[i * comps:(i + 1) * comps, :]

    def wait_sent(d, carry):
        trace_copy(d).wait_send()
        scale_copy(d).wait_send()
        return carry

    lax.fori_loop(1, n, wait_sent, 0)


def local(green_tensors, block_lists, block_count, onset_steps, slip_amount, mechanism, slip_rate):
    held, points, strains, comps, length = green_tensors.shape
    ruptures, listed = block_lists.shape
    assert ruptures == 1
    variations = onset_steps.shape[1]
    n = lax.axis_size("pts")
    cap = max(1, listed // n)
    width = points * strains * comps
    rows = points * comps
    tiles = length // LANES
    assert cap * rows <= LANES

    blocks = block_lists.reshape(listed)
    holder = blocks // held
    order = jnp.arange(listed, dtype=jnp.int32)
    rank = jnp.sum(((holder[:, None] == holder[None, :]) & (order[None, :] < order[:, None]))
                   .astype(jnp.int32), axis=1)
    lanes = jnp.arange(LANES, dtype=jnp.int32)
    hit = (holder[None, None, :] == jnp.arange(n, dtype=jnp.int32)[:, None, None]) & (
        rank[None, None, :] == (lanes % cap)[None, :, None])
    value = jnp.where((lanes < cap)[None, :, None], (blocks % held)[None, None, :],
                      (order - listed)[None, None, :])
    wants = jnp.sum(jnp.where(hit, value, 0), axis=2) + jnp.where(lanes < cap, 0, listed)[None, :]
    wants = wants.astype(jnp.int32).reshape(n, 1, LANES)

    vmem = pl.BlockSpec(memory_space=pltpu.VMEM)
    smem = pl.BlockSpec(memory_space=pltpu.SMEM)
    dma = pltpu.SemaphoreType.DMA
    seismograms = pl.pallas_call(
        functools.partial(seismogram_kernel, n, cap, points, comps, width, listed),
        out_shape=jax.ShapeDtypeStruct((variations, comps, length), jnp.float32),
        in_specs=[smem, smem, smem, vmem, vmem, vmem, vmem, vmem],
        out_specs=vmem,
        scratch_shapes=[
            pltpu.VMEM((n, 1, LANES), jnp.int32),
            pltpu.VMEM((rows, LANES), jnp.float32),
            pltpu.VMEM((n, rows, LANES), jnp.float32),
            pltpu.SMEM((n, 1, LANES), jnp.int32),
            pltpu.VMEM((n, cap, rows, length // 2), jnp.int32),
            pltpu.VMEM((n, 1, LANES), jnp.float32),
            pltpu.VMEM((n, cap, rows, length // 2), jnp.int32),
            pltpu.VMEM((n, 1, LANES), jnp.float32),
            pltpu.VMEM(((tiles + 1) * comps, variations, LANES), jnp.float32),
            pltpu.VMEM((variations, 2 * LANES, LANES), jnp.bfloat16),
            pltpu.VMEM((variations, 2 * LANES, LANES), jnp.bfloat16),
            pltpu.VMEM((listed * points, variations, LANES), jnp.int32),
            pltpu.VMEM((listed * points, variations, LANES), jnp.float32),
            dma((n,)), dma((n,)), dma((n,)), dma((n,)), dma,
            dma((n,)), dma((n,)), dma((n,)), dma((n,)),
        ],
        compiler_params=pltpu.CompilerParams(
            collective_id=0, has_side_effects=True, vmem_limit_bytes=48 << 20),
        name="seismograms",
    )(wants, mechanism, block_count, wants, green_tensors.reshape(held, width, length),
      onset_steps[0], slip_amount[0], slip_rate[0])
    return seismograms[None]


def solution(mesh):
    in_specs = (
        P(("site", "pts"), None, None, None, None),
        P(("site", "pts"), None),
        P(("site", "pts")),
        P(("site", "pts"), None, None),
        P(("site", "pts"), None, None),
        P(("site", "pts"), None),
        P(("site", "pts"), None, None),
    )
    out_specs = P(("site", "pts"), None, None, None)
    return jax.shard_map(local, mesh=mesh, in_specs=in_specs, out_specs=out_specs, check_vma=False)
```

profile of v0, /device:TPU:11, one launch (start us, length us, event | category | flops | bytes accessed | tf_op | source)
XLA Modules:
  0.0 32.6 jit_solution(11418771367258473857)
XLA Ops:
  0.7 0.7 %fusion.1 = s32[32]{0:T(128)S(1)} fusion(s32[1,32]{1,0:T(1,128)} %param.8), kind=kLoop, calls=%fused_computation.21 | loop fusion | flops 480 | bytes 256 | tf_op jit(solution)/shard_map/eq | solution.py:230
  1.3 0.7 %and_select_fusion.3 = (s32[32]{0:T(128)S(1)}, s32[32]{0:T(128)S(1)}, s32[32]{0:T(128)S(1)}) fusion(s32[1,32]{1,0:T(1,128)} %param.8), kind=kLoop, calls=%fused_computation.11 | loop fusion | flops 640 | bytes 512 | tf_op jit(solution)/shard_map/jit(floor_divide)/jit(_where)/select_n | solution.py:228
  2.0 0.2 convert_reduce_fusion
  2.2 0.1 broadcast_compare_fusion
  2.3 0.1 broadcast_select_fusion
  2.3 0.2 select_reduce_fusion
  2.5 0.0 copy-start
  2.5 0.0 copy-start.1
  2.6 0.0 copy-start.2
  2.6 0.0 copy-start.3
  2.6 2.5 %reshape.235.green_ref = bf16[16,48,1024]{2,1,0:T(8,128)(2,1)S(1)} reshape(bf16[16,4,6,2,1024]{4,3,2,1,0:T(2,128)(2,1)} %param.7) | data formatting | bytes 3145728 | tf_op jit(solution)/shard_map/reshape | solution.py:268
  5.1 0.0 copy-done
  5.1 0.0 copy-done.1
  5.1 0.0 copy-done.2
  5.1 0.0 copy-done.3
  5.1 26.8 %seismograms.1 = f32[16,2,1024]{2,1,0:T(2,128)S(1)} custom-call(s32[16,1,128]{2,1,0:T(1,128)S(1)} %broadcast_add_fusion.wants_s_ref.wants_ref, f32[1,6]{1,0:T(1,128)S(1)} %copy-done.3, s32[1]{0:T(128)S(6)} %copy.9.count_ref, s32[16,1,128]{2,1,0:T(1,128)S(1)} %broadcast_add_fusion.wants_s_ref.wants_ref, bf16[16,48,1024]{2,1,0:T(8,128)(2,1)S(1)} %reshape.235.green_ref, ...), custom_call_target="tpu_custom_call" | custom-call | tf_op jit(solution)/shard_map/seismograms/pallas_call | solution.py:243
  31.9 0.7 %copy.10 = f32[1,16,2,1024]{3,2,1,0:T(2,128)} copy(f32[1,16,2,1024]{3,2,1,0:T(2,128)S(1)} %bitcast.22) | data formatting | bytes 262144
  (5 shorter events, 0.0 us)
Async XLA Ops:
  2.5 2.6 %copy-start = (s32[1,16,128]{2,1,0:T(8,128)S(1)}, s32[1,16,128]{2,1,0:T(8,128)}, u32[]{:S(2)}) copy-start(s32[1,16,128]{2,1,0:T(8,128)} %param.10) | copy-start | bytes 24580
  2.5 2.6 %copy-start.1 = (f32[1,16,128]{2,1,0:T(8,128)S(1)}, f32[1,16,128]{2,1,0:T(8,128)}, u32[]{:S(2)}) copy-start(f32[1,16,128]{2,1,0:T(8,128)} %param.11) | copy-start | bytes 24580
  2.6 2.6 %copy-start.2 = (f32[1,16,128]{2,1,0:T(8,128)S(1)}, f32[1,16,128]{2,1,0:T(8,128)}, u32[]{:S(2)}) copy-start(f32[1,16,128]{2,1,0:T(8,128)} %param.13) | copy-start | bytes 24580
  2.6 2.6 %copy-start.3 = (f32[1,6]{1,0:T(1,128)S(1)}, f32[1,6]{1,0:T(1,128)}, u32[]{:S(2)}) copy-start(f32[1,6]{1,0:T(1,128)} %mech_s_ref.1) | copy-start | bytes 76
where the time goes:
time: 33 us; the launch traced here: 32.6 us
  Pallas kernels  26.8 us (81%)
  local copies, waits for them, and re-layouts  3.2 us (10%)
  other arithmetic  1.84 us (6%)
  between operations  0.77 us (2%)
    pallas_call x1, Pallas kernels, local(): pl.pallas_call(functools.partial(seismogram_kernel, n, cap, points, comps...  26.8 us
    reshape x1, local copies, waits for them, and re-layouts, local(): green_tensors.reshape(held, width, length)  2.51 us
    unnamed x9, local copies, waits for them, and re-layouts  0.68 us
    select_n x1, other arithmetic, local(): holder = blocks // held  0.67 us
    eq x1, other arithmetic, local(): holder[:, None] == holder[None, :]  0.67 us

commit v1 on v0

v1 whole, which is shorter than its diff:
```python
import functools

import jax
import jax.numpy as jnp
from jax import lax
from jax.experimental import pallas as pl
from jax.experimental.pallas import tpu as pltpu
from jax.sharding import PartitionSpec as P

LANES = 128
TOP = 32766.0


def seismogram_kernel(n, plane, cap, held, points, comps,
                      count_s, list_hbm, mech_hbm, green_hbm, onset_hbm, slip_hbm, rate_hbm, out_ref,
                      list_v, mech_v, mech_row, green, onset_v, slip_v, rate_v,
                      table, own_v, own_s, want_v, gain_v, outbox, out_scale, inbox, in_scale,
                      motion, high_taps, low_taps, source_of, back_of, weight_of, meta_bytes, trace_bytes,
                      local_sem, far_sem, send_m, recv_m, send_t, recv_t):
    me = lax.axis_index("pts")
    planes = n // plane
    z = me // plane
    i_own = me % plane
    toward = jnp.where(z < planes // 2, 1, -1)
    listed = list_hbm.shape[-1]
    strains = mech_hbm.shape[-1]
    variations, rows = out_ref.shape[0], out_ref.shape[1]
    tiles = rows // comps
    half = rows // 2
    mesh_id = pl.DeviceIdType.MESH

    barrier = pltpu.get_barrier_semaphore()

    def inside(q):
        return jnp.logical_and(q >= 0, q < planes)

    def in_plane(q, action):
        def body(t, carry):
            action(q * plane + (i_own + t) % plane)
            return carry

        @pl.when(inside(q))
        def _():
            lax.fori_loop(0, plane, body, 0, unroll=True)

    def beside(action):
        def body(t, carry):
            action(z * plane + (i_own + t) % plane)
            return carry

        lax.fori_loop(1, plane, body, 0, unroll=True)

    def greet(there):
        pl.semaphore_signal(barrier, inc=1, device_id={"pts": there}, device_id_type=mesh_id)

    in_plane(z + toward, greet)
    in_plane(z - toward, greet)
    beside(greet)

    local_copies = [
        pltpu.make_async_copy(src, dst, local_sem.at[i]) for i, (src, dst) in enumerate([
            (list_hbm, list_v), (mech_hbm, mech_v),
            (onset_hbm, onset_v), (slip_hbm, slip_v), (rate_hbm, rate_v), (green_hbm, green)])]
    for copy in local_copies:
        copy.start()
    for copy in local_copies[:2]:
        copy.wait()

    slots = n * cap

    def holder_of(blocks):
        if held & (held - 1) == 0:
            return jnp.right_shift(blocks, held.bit_length() - 1)
        return sum((blocks >= h * held).astype(jnp.int32) for h in range(1, n))

    k_across = lax.broadcasted_iota(jnp.int32, (listed, listed), 1)
    k_down = lax.broadcasted_iota(jnp.int32, (listed, listed), 0)
    as_row = jnp.broadcast_to(list_v[...], (listed, listed))
    as_col = jnp.sum(jnp.where(k_across == k_down, as_row, 0), axis=1, keepdims=True)
    holder_row = holder_of(as_row)
    holder_col = holder_of(as_col)
    same = holder_row == holder_col
    rank_row = jnp.sum(jnp.where(jnp.logical_and(same, k_down < k_across), 1, 0), axis=0, keepdims=True)
    rank_col = jnp.sum(jnp.where(jnp.logical_and(same, k_across < k_down), 1, 0), axis=1, keepdims=True)
    slot_down = lax.broadcasted_iota(jnp.int32, (slots, listed), 0)
    slot_row = holder_row[0:1] * cap + rank_row
    block_row = as_row[0:1] - holder_row[0:1] * held
    hit = slot_down == jnp.broadcast_to(slot_row, (slots, listed))
    block_col = jnp.sum(jnp.where(hit, jnp.broadcast_to(block_row, (slots, listed)), 0), axis=1, keepdims=True)
    block_col = jnp.broadcast_to(block_col, (slots, LANES))
    for h in range(n):
        table[h] = block_col[h * cap:(h + 1) * cap]
    mech_row[...] = jnp.zeros(mech_row.shape, jnp.float32)
    mech_row[:, 0:strains] = mech_v[...]

    has_low = jnp.where(z > 0, 1, 0)
    has_high = jnp.where(z < planes - 1, 1, 0)
    pl.semaphore_wait(barrier, plane - 1 + plane * (has_low + has_high))

    def remote(src, dst, send, recv, there):
        return pltpu.make_async_remote_copy(
            src_ref=src, dst_ref=dst, send_sem=send, recv_sem=recv,
            device_id={"pts": there}, device_id_type=mesh_id)

    def tell(k):
        for sign in (-1, 1):
            q = z + sign * k

            @pl.when(jnp.logical_and(inside(q), inside(z - sign)))
            def _():
                pl.semaphore_signal(far_sem.at[q], inc=1, device_id={"pts": me - sign * plane},
                                    device_id_type=mesh_id)

    def start_meta(there):
        remote(table.at[there], want_v.at[me], send_m, recv_m.at[z], there).start()
        remote(mech_row, gain_v.at[me], send_m, recv_m.at[z], there).start()

    def wait_meta(q):
        pltpu.make_async_copy(meta_bytes, meta_bytes, recv_m.at[q]).wait()

    def make_taps():
        i_row = lax.broadcasted_iota(jnp.int32, (LANES, LANES), 0)
        j_lane = lax.broadcasted_iota(jnp.int32, (LANES, LANES), 1)
        near_mask = j_lane >= i_row
        motion[...] = jnp.zeros(motion.shape, jnp.float32)

        def taps(v, carry):
            rate = jnp.broadcast_to(rate_v[pl.ds(v, 1), :], (LANES, LANES))
            turned = pltpu.roll(rate, 0, 1, stride=1, stride_axis=0)
            both = jnp.concatenate(
                [jnp.where(near_mask, turned, 0.0), jnp.where(near_mask, 0.0, turned)], axis=0)
            high = both.astype(jnp.bfloat16)
            high_taps[v] = high
            low_taps[v] = (both - high.astype(jnp.float32)).astype(jnp.bfloat16)
            return carry

        lax.fori_loop(0, variations, taps, 0, unroll=4)

    def spread_points():
        lane = lax.broadcasted_iota(jnp.int32, (variations, LANES), 1)
        count = count_s[0]
        onsets = onset_v[...]
        slips = slip_v[...]

        def spread(q, carry):
            pick = jnp.full((variations, LANES), q, jnp.int32)
            onset = jnp.take_along_axis(onsets, pick, axis=1)
            slip = jnp.take_along_axis(slips, pick, axis=1)
            shift = jnp.bitwise_and(onset, LANES - 1)
            source_of[q] = lane - shift
            back_of[q] = jnp.right_shift(onset, 7) + (lane >= LANES - shift).astype(jnp.int32)
            used = jnp.where(pick < count * points, 1.0, 0.0)
            weight_of[q] = slip * used
            return carry

        lax.fori_loop(0, listed * points, spread, 0, unroll=16)
        for p in range(points):
            source_of[listed * points + p] = lane
            back_of[listed * points + p] = jnp.zeros((variations, LANES), jnp.int32)
            weight_of[listed * points + p] = jnp.zeros((variations, LANES), jnp.float32)

    tell(1)
    in_plane(z + toward, start_meta)
    in_plane(z - toward, start_meta)

    def reach(k, carry):
        for sign in (-1, 1):
            q = z + sign * k

            @pl.when(inside(q))
            def _():
                pl.semaphore_wait(far_sem.at[q], 1)

        tell(k)
        in_plane(z + toward * k, start_meta)
        in_plane(z - toward * k, start_meta)
        return carry

    beside(start_meta)
    for copy in local_copies[4:5]:
        copy.wait()
    make_taps()
    if planes > 2:
        reach(2, 0)
    for copy in local_copies[2:4]:
        copy.wait()
    spread_points()
    lax.fori_loop(3, planes, reach, 0)

    as_k = lax.broadcasted_iota(jnp.int32, (listed, LANES), 0)
    lane_slot = lax.broadcasted_iota(jnp.int32, (listed, LANES), 1)
    mine = lane_slot == holder_col * cap + rank_col
    own_v[...] = jnp.sum(jnp.where(mine, as_k - listed, 0), axis=0, keepdims=True) + listed
    to_scalar = pltpu.make_async_copy(own_v, own_s, local_sem.at[6])
    to_scalar.start()
    local_copies[5].wait()

    def encode(wants, gains, box, scale_box, at):
        gain = gains
        gain = [jnp.broadcast_to(gain[:, s:s + 1], (rows, LANES)) for s in range(strains)]
        for slot in range(cap):
            block = wants[slot, 0]
            traces = []
            for p in range(points):
                total = gain[0] * green[block, p, 0].astype(jnp.float32)
                for s in range(1, strains):
                    total += gain[s] * green[block, p, s].astype(jnp.float32)
                traces.append(total)
            top = jnp.abs(traces[0])
            for part in traces[1:]:
                top = jnp.maximum(top, jnp.abs(part))
            top = jnp.max(jnp.max(top, axis=0, keepdims=True), axis=1, keepdims=True)
            top = jnp.broadcast_to(jnp.maximum(top, 1e-30), (1, LANES))
            scale_box[at, :, slot * LANES:(slot + 1) * LANES] = top * (1.0 / (TOP * 65536.0))
            inverse = jnp.broadcast_to(TOP / top, (half, LANES))
            for p in range(points):
                low = lax.round(traces[p][:half] * inverse, lax.RoundingMethod.TO_NEAREST_EVEN)
                high = lax.round(traces[p][half:] * inverse - low * (1.0 / 65536.0),
                                 lax.RoundingMethod.TO_NEAREST_EVEN)
                box[at, slot, p] = jnp.left_shift(high.astype(jnp.int32), 16) + low.astype(jnp.int32)

    def encode_to(there):
        encode(want_v[there], gain_v[there], outbox, out_scale, there)
        remote(outbox.at[there], inbox.at[me], send_t, recv_t.at[me], there).start()
        remote(out_scale.at[there], in_scale.at[me], send_t, recv_t.at[me], there).start()

    def encode_far(t, carry):
        ring = t // plane
        q = z + jnp.where(ring % 2 == 0, toward, -toward) * (ring // 2 + 1)

        @pl.when(inside(q))
        def _():
            @pl.when(t % plane == 0)
            def _():
                wait_meta(q)

            encode_to(q * plane + (i_own + t) % plane)

        return carry

    lax.fori_loop(0, 2 * (planes - 1) * plane, encode_far, 0)

    if plane > 1:
        beside_bytes = meta_bytes.at[pl.ds(0, (plane - 1) * (cap + 1))]
        pltpu.make_async_copy(beside_bytes, beside_bytes, recv_m.at[z]).wait()

    def encode_plane(t, carry):
        encode_to(z * plane + (i_own + t) % plane)
        return carry

    lax.fori_loop(1, plane, encode_plane, 0)
    encode(table[me], mech_row[...], inbox, in_scale, me)
    to_scalar.wait()

    depth = tiles // 2

    def add_traces(js):
        bases = [own_s[0, j * cap + slot] * points for j in js for slot in range(cap)]
        scales = [jnp.broadcast_to(in_scale[j, :, slot * LANES:(slot + 1) * LANES], (8, LANES))
                  for j in js for slot in range(cap)]
        for group in range(variations // 8):
            part = slice(group * 8, group * 8 + 8)
            acc = [motion[comps + q, part, :] for q in range(rows)]
            for e, (base, scale) in enumerate(zip(bases, scales)):
                j, slot = js[e // cap], e % cap
                for p in range(points):
                    source = jnp.bitwise_and(source_of[base + p, part, :], LANES - 1)
                    back = back_of[base + p, part, :]
                    weight = weight_of[base + p, part, :] * scale
                    one = back >= 1
                    two = back >= 2
                    for c in range(comps):
                        words = [jnp.broadcast_to(
                            inbox[j, slot, p, i * comps + c:i * comps + c + 1, :], (8, LANES))
                            for i in range(depth)]
                        prev2 = jnp.left_shift(words[depth - 2], 16)
                        prev1 = jnp.left_shift(words[depth - 1], 16)
                        for i in range(depth):
                            cur = words[i]
                            mixed = jnp.where(two, prev2, jnp.where(one, prev1, cur))
                            moved = jnp.take_along_axis(mixed, source, axis=1)
                            row = i * comps + c
                            acc[row] += weight * jnp.left_shift(moved, 16).astype(jnp.float32)
                            acc[row + half] += weight * moved.astype(jnp.float32)
                            prev2, prev1 = prev1, cur
            for q in range(rows):
                motion[comps + q, part, :] = acc[q]

    pair = 2 if plane % 2 == 0 else 1

    def arrive(t, carry):
        ring = t // (plane // pair)
        k = (ring + 1) // 2
        q = z + jnp.where(ring % 2 == 1, -toward, toward) * k
        first = q * plane + ((i_own // pair + t) % (plane // pair)) * pair

        @pl.when(inside(q))
        def _():
            for j in [first + d for d in range(pair)]:
                @pl.when(j != me)
                def _():
                    pltpu.make_async_copy(trace_bytes, trace_bytes, recv_t.at[j]).wait()

            add_traces([first + d for d in range(pair)])

        return carry

    lax.fori_loop(0, (2 * planes - 1) * (plane // pair), arrive, 0)

    for v in range(variations):
        lhs = jnp.concatenate([motion[comps:comps + rows, v, :], motion[0:rows, v, :]], axis=1)
        high = lhs.astype(jnp.bfloat16).astype(jnp.float32)
        pair = jnp.concatenate([high, lhs - high], axis=0).astype(jnp.bfloat16)
        main = jnp.dot(pair, high_taps[v], preferred_element_type=jnp.float32)
        minor = jnp.dot(pair[:rows], low_taps[v], preferred_element_type=jnp.float32)
        out_ref[v] = main[:rows] + (main[rows:] + minor)

    others = pl.ds(0, n - 1)
    for box, sem in ((want_v, send_m), (gain_v, send_m), (outbox, send_t), (out_scale, send_t)):
        pltpu.make_async_copy(box.at[others], box.at[others], sem).wait()


def local(plane, green_tensors, block_lists, block_count, onset_steps, slip_amount, mechanism, slip_rate):
    held, points, strains, comps, length = green_tensors.shape
    ruptures, listed = block_lists.shape
    assert ruptures == 1
    variations = onset_steps.shape[1]
    n = lax.axis_size("pts")
    cap = max(1, listed // n)
    tiles = length // LANES
    rows = tiles * comps
    assert n * cap <= LANES and listed * points <= LANES and rows == 16 and variations % 8 == 0
    green = green_tensors.reshape(held, points, strains, comps, tiles, LANES)
    green = green.transpose(0, 1, 2, 4, 3, 5).reshape(held, points, strains, rows, LANES)

    hbm = pl.BlockSpec(memory_space=pltpu.MemorySpace.HBM)
    vmem = pl.BlockSpec(memory_space=pltpu.VMEM)
    dma = pltpu.SemaphoreType.DMA
    planes = n // plane
    seismograms = pl.pallas_call(
        functools.partial(seismogram_kernel, n, plane, cap, held, points, comps),
        out_shape=jax.ShapeDtypeStruct((variations, rows, LANES), jnp.float32),
        in_specs=[pl.BlockSpec(memory_space=pltpu.SMEM)] + [hbm] * 6,
        out_specs=vmem,
        scratch_shapes=[
            pltpu.VMEM((1, listed), jnp.int32),
            pltpu.VMEM((1, strains), jnp.float32),
            pltpu.VMEM((1, LANES), jnp.float32),
            pltpu.VMEM((held, points, strains, rows, LANES), jnp.bfloat16),
            pltpu.VMEM((variations, listed * points), jnp.int32),
            pltpu.VMEM((variations, listed * points), jnp.float32),
            pltpu.VMEM((variations, LANES), jnp.float32),
            pltpu.VMEM((n, cap, LANES), jnp.int32),
            pltpu.VMEM((1, LANES), jnp.int32),
            pltpu.SMEM((1, LANES), jnp.int32),
            pltpu.VMEM((n, cap, LANES), jnp.int32),
            pltpu.VMEM((n, 1, LANES), jnp.float32),
            pltpu.VMEM((n, cap, points, rows // 2, LANES), jnp.int32),
            pltpu.VMEM((n, 1, cap * LANES), jnp.float32),
            pltpu.VMEM((n, cap, points, rows // 2, LANES), jnp.int32),
            pltpu.VMEM((n, 1, cap * LANES), jnp.float32),
            pltpu.VMEM((rows + comps, variations, LANES), jnp.float32),
            pltpu.VMEM((variations, 2 * LANES, LANES), jnp.bfloat16),
            pltpu.VMEM((variations, 2 * LANES, LANES), jnp.bfloat16),
            pltpu.VMEM(((listed + 1) * points, variations, LANES), jnp.int32),
            pltpu.VMEM(((listed + 1) * points, variations, LANES), jnp.int32),
            pltpu.VMEM(((listed + 1) * points, variations, LANES), jnp.float32),
            pltpu.VMEM((plane * (cap + 1), 1, LANES), jnp.int32),
            pltpu.VMEM((cap * (points * rows // 2 + 1), 1, LANES), jnp.int32),
            dma((7,)), pltpu.SemaphoreType.REGULAR((planes,)), dma, dma((planes,)), dma, dma((n,)),
        ],
        compiler_params=pltpu.CompilerParams(
            collective_id=0, has_side_effects=True, vmem_limit_bytes=32 << 20),
        name="seismograms",
    )(block_count, *(pltpu.with_memory_space_constraint(x, pltpu.MemorySpace.HBM) for x in (
        block_lists, mechanism, green, onset_steps[0], slip_amount[0], slip_rate[0])))
    out = seismograms.reshape(variations, tiles, comps, LANES).transpose(0, 2, 1, 3)
    return out.reshape(1, variations, comps, length)


def solution(mesh):
    n = mesh.shape["pts"]
    line = mesh.devices.reshape(-1, n)[0]
    heights = [getattr(d, "coords", (0, 0, 0))[2] for d in line]
    plane = sum(1 for h in heights if h == heights[0])
    assert n % plane == 0
    in_specs = (
        P(("site", "pts"), None, None, None, None),
        P(("site", "pts"), None),
        P(("site", "pts")),
        P(("site", "pts"), None, None),
        P(("site", "pts"), None, None),
        P(("site", "pts"), None),
        P(("site", "pts"), None, None),
    )
    out_specs = P(("site", "pts"), None, None, None)
    return jax.shard_map(functools.partial(local, plane), mesh=mesh, in_specs=in_specs, out_specs=out_specs,
                         check_vma=False)
```

time: 33 us -> 25.7 us (0.78)
  the two profiles are of different devices: /device:TPU:11 before, /device:TPU:0 now
where the time goes in v1:
time: 25.7 us; the launch traced here: 25.6 us
  Pallas kernels  24.3 us (95%)
  local copies, waits for them, and re-layouts  0.66 us (3%)
  between operations  0.66 us (3%)
    pallas_call x1, Pallas kernels, local(): pl.pallas_call(functools.partial(seismogram_kernel, n, plane, cap, held,...  24.3 us
    unnamed x1, local copies, waits for them, and re-layouts  0.66 us

profile of v1, /device:TPU:0, one launch (start us, length us, event | category | flops | bytes accessed | tf_op | source)
XLA Modules:
  0.0 25.6 jit_solution(11866310489212177233)
XLA Ops:
  0.7 24.3 %seismograms.1 = f32[16,16,128]{2,1,0:T(8,128)S(1)} custom-call(s32[1]{0:T(128)S(6)} %copy.11.count_s, s32[1,32]{1,0:T(1,128)} %list_hbm.1, f32[1,6]{1,0:T(1,128)} %mech_hbm.1, bf16[16,4,6,16,128]{4,3,2,1,0:T(8,128)(2,1)} %bitcast.14, s32[16,128]{1,0:T(8,128)} %bitcast.15, f32[16,128]{1,0:T(8,128)} %bitcast.16, f32[16,128]{1,0:T(8,128)} %bitcast.17), custom_call_target="tpu_custom_call" | custom-call | tf_op jit(solution)/shard_map/seismograms/pallas_call | solution.py:340
  24.9 0.7 %copy.12 = f32[1,16,2,1024]{3,2,1,0:T(2,128)} copy(f32[1,16,2,1024]{3,2,1,0:T(2,128)S(1)} %bitcast.13) | data formatting | bytes 262144

commit v2 on v1

v2 whole, which is shorter than its diff:
```python
import functools

import jax
import jax.numpy as jnp
from jax import lax
from jax.experimental import pallas as pl
from jax.experimental.pallas import tpu as pltpu
from jax.sharding import PartitionSpec as P

LANES = 128
TOP = 32766.0
SLIP = 32767.0


def seismogram_kernel(n, plane, cap, held, points, comps,
                      count_s, list_hbm, mech_hbm, green_hbm, onset_hbm, slip_hbm, rate_hbm, out_ref,
                      list_v, mech_v, mech_row, green, onset_v, slip_v, rate_v,
                      table, want_v, gain_v, word_out, word_in, box, scale_box, sum_out, sum_in, top_out, top_in,
                      total, motion, high_taps, low_taps, source_of, back_of, weight_of, meta_bytes, trace_bytes,
                      sum_bytes, local_sem, far_sem, send_m, recv_m, send_w, recv_w, send_t, recv_t, send_p, recv_p):
    me = lax.axis_index("pts")
    planes = n // plane
    z = me // plane
    i_own = me % plane
    toward = jnp.where(z < planes // 2, 1, -1)
    listed = list_hbm.shape[-1]
    strains = mech_hbm.shape[-1]
    variations, rows = out_ref.shape[0], out_ref.shape[1]
    tiles = rows // comps
    half = rows // 2
    depth = tiles // 2
    width = plane * cap * points
    fold = LANES // width
    folded = variations // fold
    mesh_id = pl.DeviceIdType.MESH
    nearest = lax.RoundingMethod.TO_NEAREST_EVEN

    barrier = pltpu.get_barrier_semaphore()

    def inside(q):
        return jnp.logical_and(q >= 0, q < planes)

    def in_plane(q, action):
        def body(t, carry):
            action(q * plane + (i_own + t) % plane)
            return carry

        @pl.when(inside(q))
        def _():
            lax.fori_loop(0, plane, body, 0, unroll=True)

    def beside(action):
        def body(t, carry):
            action(z * plane + (i_own + t) % plane)
            return carry

        lax.fori_loop(1, plane, body, 0, unroll=True)

    def greet(there):
        pl.semaphore_signal(barrier, inc=1, device_id={"pts": there}, device_id_type=mesh_id)

    in_plane(z + toward, greet)
    in_plane(z - toward, greet)
    beside(greet)

    local_copies = [
        pltpu.make_async_copy(src, dst, local_sem.at[i]) for i, (src, dst) in enumerate([
            (list_hbm, list_v), (mech_hbm, mech_v),
            (onset_hbm, onset_v), (slip_hbm, slip_v), (rate_hbm, rate_v), (green_hbm, green)])]
    for copy in local_copies:
        copy.start()
    for copy in local_copies[:2]:
        copy.wait()

    slots = n * cap

    def holder_of(blocks):
        if held & (held - 1) == 0:
            return jnp.right_shift(blocks, held.bit_length() - 1)
        return sum((blocks >= h * held).astype(jnp.int32) for h in range(1, n))

    k_across = lax.broadcasted_iota(jnp.int32, (listed, listed), 1)
    k_down = lax.broadcasted_iota(jnp.int32, (listed, listed), 0)
    as_row = jnp.broadcast_to(list_v[...], (listed, listed))
    as_col = jnp.sum(jnp.where(k_across == k_down, as_row, 0), axis=1, keepdims=True)
    holder_row = holder_of(as_row)
    holder_col = holder_of(as_col)
    same = holder_row == holder_col
    rank_row = jnp.sum(jnp.where(jnp.logical_and(same, k_down < k_across), 1, 0), axis=0, keepdims=True)
    rank_col = jnp.sum(jnp.where(jnp.logical_and(same, k_across < k_down), 1, 0), axis=1, keepdims=True)
    slot_down = lax.broadcasted_iota(jnp.int32, (slots, listed), 0)
    slot_row = holder_row[0:1] * cap + rank_row
    block_row = as_row[0:1] - holder_row[0:1] * held
    hit = slot_down == jnp.broadcast_to(slot_row, (slots, listed))
    block_col = jnp.sum(jnp.where(hit, jnp.broadcast_to(block_row, (slots, listed)), 0), axis=1, keepdims=True)
    block_col = jnp.broadcast_to(block_col, (slots, LANES))
    for h in range(n):
        table[h] = block_col[h * cap:(h + 1) * cap]
    mech_row[...] = jnp.zeros(mech_row.shape, jnp.float32)
    mech_row[:, 0:strains] = mech_v[...]

    has_low = jnp.where(z > 0, 1, 0)
    has_high = jnp.where(z < planes - 1, 1, 0)
    pl.semaphore_wait(barrier, plane - 1 + plane * (has_low + has_high))

    def remote(src, dst, send, recv, there):
        return pltpu.make_async_remote_copy(
            src_ref=src, dst_ref=dst, send_sem=send, recv_sem=recv,
            device_id={"pts": there}, device_id_type=mesh_id)

    def await_bytes(ref, sem):
        pltpu.make_async_copy(ref, ref, sem).wait()

    def tell(k):
        for sign in (-1, 1):
            q = z + sign * k

            @pl.when(jnp.logical_and(inside(q), inside(z - sign)))
            def _():
                pl.semaphore_signal(far_sem.at[q], inc=1, device_id={"pts": me - sign * plane},
                                    device_id_type=mesh_id)

    def start_meta(there):
        remote(table.at[there], want_v.at[me], send_m, recv_m.at[z], there).start()
        remote(mech_row, gain_v.at[me], send_m, recv_m.at[z], there).start()

    def start_words(q):
        @pl.when(inside(q))
        def _():
            remote(word_out.at[q], word_in.at[z], send_w, recv_w.at[z], q * plane + i_own).start()

    tell(1)
    in_plane(z + toward, start_meta)
    in_plane(z - toward, start_meta)
    beside(start_meta)
    want_v[me] = table[me]
    gain_v[me] = mech_row[...]

    def make_words():
        lane = lax.broadcasted_iota(jnp.int32, (1, LANES), 1)
        as_k = lax.broadcasted_iota(jnp.int32, (listed, LANES), 0)
        entry = jnp.bitwise_and(lane, width - 1)
        in_slot = jnp.right_shift(entry, points.bit_length() - 1)
        slot_col = jnp.broadcast_to(holder_col * cap + rank_col, (listed, LANES))
        slip = lax.round(slip_v[...] * SLIP, nearest).astype(jnp.int32)
        packed = jnp.bitwise_or(jnp.left_shift(onset_v[...], 16), slip)
        count = count_s[0]
        for q in range(planes):
            mine = slot_col == jnp.broadcast_to(in_slot + q * plane * cap, (listed, LANES))
            k = jnp.sum(jnp.where(mine, as_k - listed, 0), axis=0, keepdims=True) + listed
            pick = jnp.minimum(k, listed - 1) * points + jnp.bitwise_and(entry, points - 1)
            words = jnp.take_along_axis(packed, jnp.broadcast_to(pick, (variations, LANES)), axis=1)
            words = jnp.where(jnp.broadcast_to(k < count, (variations, LANES)), words, 0)
            kept = words[0:folded]
            for b in range(1, fold):
                there = jnp.broadcast_to(lane >= b * width, (folded, LANES))
                kept = jnp.where(there, words[b * folded:(b + 1) * folded], kept)
            word_out[q] = kept
        word_in[z] = word_out[z]

    def make_taps():
        i_row = lax.broadcasted_iota(jnp.int32, (LANES, LANES), 0)
        j_lane = lax.broadcasted_iota(jnp.int32, (LANES, LANES), 1)
        near_mask = j_lane >= i_row

        def taps(v, carry):
            rate = jnp.broadcast_to(rate_v[pl.ds(v, 1), :], (LANES, LANES))
            turned = pltpu.roll(rate, 0, 1, stride=1, stride_axis=0)
            both = jnp.concatenate(
                [jnp.where(near_mask, turned, 0.0), jnp.where(near_mask, 0.0, turned)], axis=0)
            high = both.astype(jnp.bfloat16)
            high_taps[v] = high
            low_taps[v] = (both - high.astype(jnp.float32)).astype(jnp.bfloat16)
            return carry

        lax.fori_loop(0, variations, taps, 0, unroll=4)

    def reach(k, carry):
        for sign in (-1, 1):
            q = z + sign * k

            @pl.when(inside(q))
            def _():
                pl.semaphore_wait(far_sem.at[q], 1)

        tell(k)
        in_plane(z + toward * k, start_meta)
        in_plane(z - toward * k, start_meta)
        start_words(z + toward * k)
        start_words(z - toward * k)
        return carry

    for copy in local_copies[2:4]:
        copy.wait()
    make_words()
    start_words(z + toward)
    start_words(z - toward)
    if planes > 2:
        reach(2, 0)
    local_copies[4].wait()
    make_taps()
    motion[0:comps] = jnp.zeros((comps, variations, LANES), jnp.float32)
    lax.fori_loop(3, planes, reach, 0)
    local_copies[5].wait()

    def encode(r, at):
        gain = gain_v[r]
        gain = [jnp.broadcast_to(gain[:, s:s + 1], (rows, LANES)) for s in range(strains)]
        wants = want_v[r]
        for slot in range(cap):
            block = wants[slot, 0]
            traces = []
            for p in range(points):
                trace = gain[0] * green[block, p, 0].astype(jnp.float32)
                for s in range(1, strains):
                    trace += gain[s] * green[block, p, s].astype(jnp.float32)
                traces.append(trace)
            top = jnp.abs(traces[0])
            for part in traces[1:]:
                top = jnp.maximum(top, jnp.abs(part))
            top = jnp.max(jnp.max(top, axis=0, keepdims=True), axis=1, keepdims=True)
            top = jnp.broadcast_to(jnp.maximum(top, 1e-30), (1, LANES))
            scale_box[at, :, slot * LANES:(slot + 1) * LANES] = top * (1.0 / (TOP * 65536.0))
            inverse = jnp.broadcast_to(TOP / top, (half, LANES))
            for p in range(points):
                low = lax.round(traces[p][:half] * inverse, nearest)
                high = lax.round(traces[p][half:] * inverse - low * (1.0 / 65536.0), nearest)
                box[at, slot, p] = jnp.left_shift(high.astype(jnp.int32), 16) + low.astype(jnp.int32)

    last_ring = 2 * (planes - 1)

    def plane_of(ring):
        k = jnp.where(ring == last_ring, 0, ring // 2 + 1)
        return z + jnp.where(ring % 2 == 0, toward, -toward) * k

    def encode_all(t, carry):
        ring = t // plane
        q = plane_of(ring)

        @pl.when(inside(q))
        def _():
            @pl.when(jnp.logical_and(t % plane == 0, q != z))
            def _():
                await_bytes(meta_bytes, recv_m.at[q])

            if plane > 1:
                @pl.when(jnp.logical_and(t % plane == 0, q == z))
                def _():
                    await_bytes(meta_bytes.at[pl.ds(0, (plane - 1) * (cap + 1))], recv_m.at[q])

            i = (i_own + t + 1) % plane
            r = q * plane + i
            encode(r, jnp.where(i == i_own, r + n, r))

            @pl.when(i != i_own)
            def _():
                there = z * plane + i
                slot = q * plane + i_own
                remote(box.at[r], box.at[n + slot], send_t, recv_t.at[slot], there).start()
                remote(scale_box.at[r], scale_box.at[n + slot], send_t, recv_t.at[slot], there).start()

        return carry

    lax.fori_loop(0, (2 * planes - 1) * plane, encode_all, 0)

    def spread(q):
        words = word_in[q]
        words = jnp.concatenate([words] * fold, axis=0)
        lane = lax.broadcasted_iota(jnp.int32, (variations, LANES), 1)
        start = lax.broadcasted_iota(jnp.int32, (variations, LANES), 0) // folded * width
        for e in range(width):
            word = jnp.take_along_axis(words, start + e, axis=1)
            onset = jnp.right_shift(word, 16)
            shift = jnp.bitwise_and(onset, LANES - 1)
            source_of[e] = lane - shift
            back_of[e] = jnp.right_shift(onset, 7) + (lane >= LANES - shift).astype(jnp.int32)
            weight_of[e] = jnp.bitwise_and(word, 0xFFFF).astype(jnp.float32) * (1.0 / SLIP)

    pair = 2 if plane % 2 == 0 else 1

    def add_traces(q, i_first):
        for group in range(variations // 8):
            part = slice(group * 8, group * 8 + 8)
            acc = [total[r, part, :] for r in range(rows)]
            for e in range(pair * cap):
                at = n + q * plane + i_first + e // cap
                slot = e % cap
                scale = jnp.broadcast_to(scale_box[at, :, slot * LANES:(slot + 1) * LANES], (8, LANES))
                for p in range(points):
                    entry = (i_first * cap + e) * points + p
                    source = jnp.bitwise_and(source_of[entry, part, :], LANES - 1)
                    back = back_of[entry, part, :]
                    weight = weight_of[entry, part, :] * scale
                    one = back >= 1
                    two = back >= 2
                    for c in range(comps):
                        words = [jnp.broadcast_to(
                            box[at, slot, p, i * comps + c:i * comps + c + 1, :], (8, LANES))
                            for i in range(depth)]
                        prev2 = jnp.left_shift(words[depth - 2], 16)
                        prev1 = jnp.left_shift(words[depth - 1], 16)
                        for i in range(depth):
                            cur = words[i]
                            mixed = jnp.where(two, prev2, jnp.where(one, prev1, cur))
                            moved = jnp.take_along_axis(mixed, source, axis=1)
                            row = i * comps + c
                            acc[row] += weight * jnp.left_shift(moved, 16).astype(jnp.float32)
                            acc[row + half] += weight * moved.astype(jnp.float32)
                            prev2, prev1 = prev1, cur
            for r in range(rows):
                total[r, part, :] = acc[r]

    def send_sum(q):
        top = jnp.abs(total[0])
        for r in range(1, rows):
            top = jnp.maximum(top, jnp.abs(total[r]))
        top = jnp.maximum(jnp.max(top, axis=0, keepdims=True), 1e-30)
        top_out[q] = top * (1.0 / (TOP * 65536.0))
        inverse = jnp.broadcast_to(TOP / top, (variations, LANES))
        for r in range(half):
            low = lax.round(total[r] * inverse, nearest)
            high = lax.round(total[r + half] * inverse - low * (1.0 / 65536.0), nearest)
            sum_out[q, r] = jnp.left_shift(high.astype(jnp.int32), 16) + low.astype(jnp.int32)
        there = q * plane + i_own
        remote(sum_out.at[q], sum_in.at[z], send_p, recv_p.at[z], there).start()
        remote(top_out.at[q], top_in.at[z], send_p, recv_p.at[z], there).start()

    def sum_plane(ring, carry):
        q = plane_of(ring)

        @pl.when(inside(q))
        def _():
            @pl.when(q != z)
            def _():
                await_bytes(word_in.at[q], recv_w.at[q])

            spread(q)
            total[...] = jnp.zeros(total.shape, jnp.float32)

            def sources(t, carry):
                i_first = ((i_own // pair + t + 1) % (plane // pair)) * pair
                for d in range(pair):
                    @pl.when(i_first + d != i_own)
                    def _():
                        await_bytes(trace_bytes, recv_t.at[q * plane + i_first + d])

                add_traces(q, i_first)
                return carry

            lax.fori_loop(0, plane // pair, sources, 0)

            @pl.when(q != z)
            def _():
                send_sum(q)

            @pl.when(q == z)
            def _():
                motion[comps:comps + rows] = total[...]

        return carry

    lax.fori_loop(0, last_ring + 1, sum_plane, 0)

    def add_sum(t, carry):
        ring = jnp.bitwise_xor(t, 1)
        q = plane_of(ring)

        @pl.when(inside(q))
        def _():
            await_bytes(sum_bytes, recv_p.at[q])
            scale = jnp.broadcast_to(top_in[q], (variations, LANES))
            for r in range(half):
                word = sum_in[q, r]
                motion[comps + r] += jnp.left_shift(word, 16).astype(jnp.float32) * scale
                motion[comps + r + half] += word.astype(jnp.float32) * scale

        return carry

    lax.fori_loop(0, last_ring, add_sum, 0)

    for v in range(variations):
        lhs = jnp.concatenate([motion[comps:comps + rows, v, :], motion[0:rows, v, :]], axis=1)
        high = lhs.astype(jnp.bfloat16).astype(jnp.float32)
        pair_rows = jnp.concatenate([high, lhs - high], axis=0).astype(jnp.bfloat16)
        main = jnp.dot(pair_rows, high_taps[v], preferred_element_type=jnp.float32)
        minor = jnp.dot(pair_rows[:rows], low_taps[v], preferred_element_type=jnp.float32)
        out_ref[v] = main[:rows] + (main[rows:] + minor)

    others = pl.ds(0, n - 1)
    for ref, sem in ((want_v.at[others], send_m), (gain_v.at[others], send_m)):
        await_bytes(ref, sem)
    sent = pl.ds(0, planes * (plane - 1))
    if plane > 1:
        for ref in (box.at[sent], scale_box.at[sent]):
            await_bytes(ref, send_t)
    if planes > 1:
        far = pl.ds(0, planes - 1)
        await_bytes(word_in.at[far], send_w)
        for ref in (sum_in.at[far], top_in.at[far]):
            await_bytes(ref, send_p)


def local(plane, green_tensors, block_lists, block_count, onset_steps, slip_amount, mechanism, slip_rate):
    held, points, strains, comps, length = green_tensors.shape
    ruptures, listed = block_lists.shape
    assert ruptures == 1
    variations = onset_steps.shape[1]
    n = lax.axis_size("pts")
    cap = max(1, listed // n)
    tiles = length // LANES
    rows = tiles * comps
    planes = n // plane
    width = plane * cap * points
    fold = LANES // width
    assert listed * points <= LANES and rows == 16 and variations % 8 == 0
    assert fold * width == LANES and variations % fold == 0 and points & (points - 1) == 0
    green = green_tensors.reshape(held, points, strains, comps, tiles, LANES)
    green = green.transpose(0, 1, 2, 4, 3, 5).reshape(held, points, strains, rows, LANES)

    hbm = pl.BlockSpec(memory_space=pltpu.MemorySpace.HBM)
    vmem = pl.BlockSpec(memory_space=pltpu.VMEM)
    dma = pltpu.SemaphoreType.DMA
    i32, f32 = jnp.int32, jnp.float32
    seismograms = pl.pallas_call(
        functools.partial(seismogram_kernel, n, plane, cap, held, points, comps),
        out_shape=jax.ShapeDtypeStruct((variations, rows, LANES), f32),
        in_specs=[pl.BlockSpec(memory_space=pltpu.SMEM)] + [hbm] * 6,
        out_specs=vmem,
        scratch_shapes=[
            pltpu.VMEM((1, listed), i32),
            pltpu.VMEM((1, strains), f32),
            pltpu.VMEM((1, LANES), f32),
            pltpu.VMEM((held, points, strains, rows, LANES), jnp.bfloat16),
            pltpu.VMEM((variations, listed * points), i32),
            pltpu.VMEM((variations, listed * points), f32),
            pltpu.VMEM((variations, LANES), f32),
            pltpu.VMEM((n, cap, LANES), i32),
            pltpu.VMEM((n, cap, LANES), i32),
            pltpu.VMEM((n, 1, LANES), f32),
            pltpu.VMEM((planes, variations // fold, LANES), i32),
            pltpu.VMEM((planes, variations // fold, LANES), i32),
            pltpu.VMEM((2 * n, cap, points, rows // 2, LANES), i32),
            pltpu.VMEM((2 * n, 1, cap * LANES), f32),
            pltpu.VMEM((planes, rows // 2, variations, LANES), i32),
            pltpu.VMEM((planes, rows // 2, variations, LANES), i32),
            pltpu.VMEM((planes, 1, LANES), f32),
            pltpu.VMEM((planes, 1, LANES), f32),
            pltpu.VMEM((rows, variations, LANES), f32),
            pltpu.VMEM((rows + comps, variations, LANES), f32),
            pltpu.VMEM((variations, 2 * LANES, LANES), jnp.bfloat16),
            pltpu.VMEM((variations, 2 * LANES, LANES), jnp.bfloat16),
            pltpu.VMEM((width, variations, LANES), i32),
            pltpu.VMEM((width, variations, LANES), i32),
            pltpu.VMEM((width, variations, LANES), f32),
            pltpu.VMEM((plane * (cap + 1), 1, LANES), i32),
            pltpu.VMEM((cap * (points * rows // 2 + 1), 1, LANES), i32),
            pltpu.VMEM((rows // 2 * variations + 1, 1, LANES), i32),
            dma((6,)), pltpu.SemaphoreType.REGULAR((planes,)), dma, dma((planes,)), dma, dma((planes,)),
            dma, dma((n,)), dma, dma((planes,)),
        ],
        compiler_params=pltpu.CompilerParams(
            collective_id=0, has_side_effects=True, vmem_limit_bytes=32 << 20),
        name="seismograms",
    )(block_count, *(pltpu.with_memory_space_constraint(x, pltpu.MemorySpace.HBM) for x in (
        block_lists, mechanism, green, onset_steps[0], slip_amount[0], slip_rate[0])))
    out = seismograms.reshape(variations, tiles, comps, LANES).transpose(0, 2, 1, 3)
    return out.reshape(1, variations, comps, length)


def solution(mesh):
    n = mesh.shape["pts"]
    line = mesh.devices.reshape(-1, n)[0]
    heights = [getattr(d, "coords", (0, 0, 0))[2] for d in line]
    plane = sum(1 for h in heights if h == heights[0])
    assert n % plane == 0
    in_specs = (
        P(("site", "pts"), None, None, None, None),
        P(("site", "pts"), None),
        P(("site", "pts")),
        P(("site", "pts"), None, None),
        P(("site", "pts"), None, None),
        P(("site", "pts"), None),
        P(("site", "pts"), None, None),
    )
    out_specs = P(("site", "pts"), None, None, None)
    return jax.shard_map(functools.partial(local, plane), mesh=mesh, in_specs=in_specs, out_specs=out_specs,
                         check_vma=False)
```

time: 25.7 us -> 24.8 us (0.965)
  Pallas kernels: 24.3 us -> 23.3 us
    pallas_call x1, Pallas kernels: 24.3 us -> 23.3 us  [local(): pl.pallas_call(functools.partial(seismogram_kernel, n, plane, cap, held,...]
where the time goes in v2:
time: 24.8 us; the launch traced here: 24.6 us
  Pallas kernels  23.3 us (94%)
  local copies, waits for them, and re-layouts  0.66 us (3%)
  between operations  0.66 us (3%)
    pallas_call x1, Pallas kernels, local(): pl.pallas_call(functools.partial(seismogram_kernel, n, plane, cap, held,...  23.3 us
    unnamed x1, local copies, waits for them, and re-layouts  0.66 us

profile of v2, /device:TPU:0, one launch (start us, length us, event | category | flops | bytes accessed | tf_op | source)
XLA Modules:
  0.0 24.6 jit_solution(14418325382059403866)
XLA Ops:
  0.7 23.3 %seismograms.1 = f32[16,16,128]{2,1,0:T(8,128)S(1)} custom-call(s32[1]{0:T(128)S(6)} %copy.11.count_s, s32[1,32]{1,0:T(1,128)} %list_hbm.1, f32[1,6]{1,0:T(1,128)} %mech_hbm.1, bf16[16,4,6,16,128]{4,3,2,1,0:T(8,128)(2,1)} %bitcast.14, s32[16,128]{1,0:T(8,128)} %bitcast.15, f32[16,128]{1,0:T(8,128)} %bitcast.16, f32[16,128]{1,0:T(8,128)} %bitcast.17), custom_call_target="tpu_custom_call" | custom-call | tf_op jit(solution)/shard_map/seismograms/pallas_call | solution.py:424
  24.0 0.7 %copy.12 = f32[1,16,2,1024]{3,2,1,0:T(2,128)} copy(f32[1,16,2,1024]{3,2,1,0:T(2,128)S(1)} %bitcast.13) | data formatting | bytes 262144

commit v3 on v1

--- a/solution.py
+++ b/solution.py
@@ -53,16 +53,16 @@
     def greet(there):
         pl.semaphore_signal(barrier, inc=1, device_id={"pts": there}, device_id_type=mesh_id)
 
-    in_plane(z + toward, greet)
-    in_plane(z - toward, greet)
-    beside(greet)
-
     local_copies = [
         pltpu.make_async_copy(src, dst, local_sem.at[i]) for i, (src, dst) in enumerate([
             (list_hbm, list_v), (mech_hbm, mech_v),
             (onset_hbm, onset_v), (slip_hbm, slip_v), (rate_hbm, rate_v), (green_hbm, green)])]
     for copy in local_copies:
         copy.start()
+    in_plane(z + toward, greet)
+    in_plane(z - toward, greet)
+    beside(greet)
+
     for copy in local_copies[:2]:
         copy.wait()
 
@@ -196,8 +196,9 @@
     local_copies[5].wait()
 
     def encode(wants, gains, box, scale_box, at):
-        gain = gains
-        gain = [jnp.broadcast_to(gain[:, s:s + 1], (rows, LANES)) for s in range(strains)]
+        gain = [jnp.broadcast_to(gains[:, s:s + 1], (rows, LANES)) for s in range(strains)]
+        lane_row = lax.broadcasted_iota(jnp.int32, (1, LANES), 1)
+        scales = jnp.zeros((1, LANES), jnp.float32)
         for slot in range(cap):
             block = wants[slot, 0]
             traces = []
@@ -211,52 +212,62 @@
                 top = jnp.maximum(top, jnp.abs(part))
             top = jnp.max(jnp.max(top, axis=0, keepdims=True), axis=1, keepdims=True)
             top = jnp.broadcast_to(jnp.maximum(top, 1e-30), (1, LANES))
-            scale_box[at, :, slot * LANES:(slot + 1) * LANES] = top * (1.0 / (TOP * 65536.0))
+            scales = jnp.where(lane_row >= slot * (LANES // cap), top * (1.0 / (TOP * 65536.0)), scales)
             inverse = jnp.broadcast_to(TOP / top, (half, LANES))
             for p in range(points):
                 low = lax.round(traces[p][:half] * inverse, lax.RoundingMethod.TO_NEAREST_EVEN)
                 high = lax.round(traces[p][half:] * inverse - low * (1.0 / 65536.0),
                                  lax.RoundingMethod.TO_NEAREST_EVEN)
                 box[at, slot, p] = jnp.left_shift(high.astype(jnp.int32), 16) + low.astype(jnp.int32)
+        scale_box[at] = scales
 
     def encode_to(there):
         encode(want_v[there], gain_v[there], outbox, out_scale, there)
-        remote(outbox.at[there], inbox.at[me], send_t, recv_t.at[me], there).start()
-        remote(out_scale.at[there], in_scale.at[me], send_t, recv_t.at[me], there).start()
-
-    def encode_far(t, carry):
-        ring = t // plane
-        q = z + jnp.where(ring % 2 == 0, toward, -toward) * (ring // 2 + 1)
+        remote(outbox.at[there], inbox.at[me], send_t, recv_t.at[me // 2], there).start()
+        remote(out_scale.at[there], in_scale.at[me], send_t, recv_t.at[me // 2], there).start()
+
+    chip = plane // 2
+    steps = 4 * planes - 2
+
+    def encode_step(u, carry):
+        middle = u >= 6
+        k = jnp.where(middle, planes - 1 - (u - 6) // 4, jnp.where(u >= 4, 0, 1))
+        away = jnp.where(middle, (u - 6) % 4 >= 2, jnp.logical_or(u == 1, u == 2))
+        part = jnp.where(middle, (u - 6) % 2, jnp.logical_or(jnp.logical_or(u == 2, u == 3), u == 5).astype(jnp.int32))
+        q = z + jnp.where(away, -toward, toward) * k
 
         @pl.when(inside(q))
         def _():
-            @pl.when(t % plane == 0)
+            @pl.when(jnp.logical_and(part == 0, k > 0))
             def _():
                 wait_meta(q)
 
-            encode_to(q * plane + (i_own + t) % plane)
+            @pl.when(jnp.logical_and(part == 0, k == 0))
+            def _():
+                beside_bytes = meta_bytes.at[pl.ds(0, (plane - 1) * (cap + 1))]
+                pltpu.make_async_copy(beside_bytes, beside_bytes, recv_m.at[z]).wait()
+
+            def one(t, carry):
+                there = q * plane + (i_own // chip * chip + part * chip + t) % plane
+
+                @pl.when(there != me)
+                def _():
+                    encode_to(there)
+
+                return carry
+
+            lax.fori_loop(0, chip, one, 0)
 
         return carry
 
-    lax.fori_loop(0, 2 * (planes - 1) * plane, encode_far, 0)
-
-    if plane > 1:
-        beside_bytes = meta_bytes.at[pl.ds(0, (plane - 1) * (cap + 1))]
-        pltpu.make_async_copy(beside_bytes, beside_bytes, recv_m.at[z]).wait()
-
-    def encode_plane(t, carry):
-        encode_to(z * plane + (i_own + t) % plane)
-        return carry
-
-    lax.fori_loop(1, plane, encode_plane, 0)
-    encode(table[me], mech_row[...], inbox, in_scale, me)
-    to_scalar.wait()
+    def encode_own():
+        encode(table[me], mech_row[...], inbox, in_scale, me)
 
     depth = tiles // 2
 
     def add_traces(js):
         bases = [own_s[0, j * cap + slot] * points for j in js for slot in range(cap)]
-        scales = [jnp.broadcast_to(in_scale[j, :, slot * LANES:(slot + 1) * LANES], (8, LANES))
+        scales = [jnp.broadcast_to(in_scale[j][:, slot * (LANES // cap):slot * (LANES // cap) + 1], (8, LANES))
                   for j in js for slot in range(cap)]
         for group in range(variations // 8):
             part = slice(group * 8, group * 8 + 8)
@@ -286,26 +297,34 @@
             for q in range(rows):
                 motion[comps + q, part, :] = acc[q]
 
-    pair = 2 if plane % 2 == 0 else 1
-
     def arrive(t, carry):
-        ring = t // (plane // pair)
+        ring = t // chip
         k = (ring + 1) // 2
         q = z + jnp.where(ring % 2 == 1, -toward, toward) * k
-        first = q * plane + ((i_own // pair + t) % (plane // pair)) * pair
+        first = q * plane + ((i_own // 2 + t) % chip) * 2
 
         @pl.when(inside(q))
         def _():
-            for j in [first + d for d in range(pair)]:
-                @pl.when(j != me)
-                def _():
-                    pltpu.make_async_copy(trace_bytes, trace_bytes, recv_t.at[j]).wait()
-
-            add_traces([first + d for d in range(pair)])
+            @pl.when(first == me // 2 * 2)
+            def _():
+                mate = trace_bytes.at[pl.ds(0, cap * points * half + 1)]
+                pltpu.make_async_copy(mate, mate, recv_t.at[first // 2]).wait()
+
+            @pl.when(first != me // 2 * 2)
+            def _():
+                pltpu.make_async_copy(trace_bytes, trace_bytes, recv_t.at[first // 2]).wait()
+
+            add_traces([first, first + 1])
 
         return carry
 
-    lax.fori_loop(0, (2 * planes - 1) * (plane // pair), arrive, 0)
+    lax.fori_loop(0, 6, encode_step, 0)
+    encode_own()
+    to_scalar.wait()
+    early = jnp.where(inside(z + toward * (planes - 1)), chip, 0)
+    lax.fori_loop(0, early, arrive, 0)
+    lax.fori_loop(6, steps, encode_step, 0)
+    lax.fori_loop(early, (2 * planes - 1) * chip, arrive, 0)
 
     for v in range(variations):
         lhs = jnp.concatenate([motion[comps:comps + rows, v, :], motion[0:rows, v, :]], axis=1)
@@ -356,9 +375,9 @@
             pltpu.VMEM((n, cap, LANES), jnp.int32),
             pltpu.VMEM((n, 1, LANES), jnp.float32),
             pltpu.VMEM((n, cap, points, rows // 2, LANES), jnp.int32),
-            pltpu.VMEM((n, 1, cap * LANES), jnp.float32),
+            pltpu.VMEM((n, 1, LANES), jnp.float32),
             pltpu.VMEM((n, cap, points, rows // 2, LANES), jnp.int32),
-            pltpu.VMEM((n, 1, cap * LANES), jnp.float32),
+            pltpu.VMEM((n, 1, LANES), jnp.float32),
             pltpu.VMEM((rows + comps, variations, LANES), jnp.float32),
             pltpu.VMEM((variations, 2 * LANES, LANES), jnp.bfloat16),
             pltpu.VMEM((variations, 2 * LANES, LANES), jnp.bfloat16),
@@ -366,8 +385,8 @@
             pltpu.VMEM(((listed + 1) * points, variations, LANES), jnp.int32),
             pltpu.VMEM(((listed + 1) * points, variations, LANES), jnp.float32),
             pltpu.VMEM((plane * (cap + 1), 1, LANES), jnp.int32),
-            pltpu.VMEM((cap * (points * rows // 2 + 1), 1, LANES), jnp.int32),
-            dma((7,)), pltpu.SemaphoreType.REGULAR((planes,)), dma, dma((planes,)), dma, dma((n,)),
+            pltpu.VMEM((2 * (cap * points * rows // 2 + 1), 1, LANES), jnp.int32),
+            dma((7,)), pltpu.SemaphoreType.REGULAR((planes,)), dma, dma((planes,)), dma, dma((n // 2,)),
         ],
         compiler_params=pltpu.CompilerParams(
             collective_id=0, has_side_effects=True, vmem_limit_bytes=32 << 20),
@@ -383,7 +402,7 @@
     line = mesh.devices.reshape(-1, n)[0]
     heights = [getattr(d, "coords", (0, 0, 0))[2] for d in line]
     plane = sum(1 for h in heights if h == heights[0])
-    assert n % plane == 0
+    assert n % plane == 0 and plane % 2 == 0
     in_specs = (
         P(("site", "pts"), None, None, None, None),
         P(("site", "pts"), None),

time: 25.7 us -> 24.1 us (0.938)
  the two profiles are of different devices: /device:TPU:0 before, /device:TPU:11 now
where the time goes in v3:
time: 24.1 us; the launch traced here: 23.8 us
  Pallas kernels  22.5 us (93%)
  local copies, waits for them, and re-layouts  0.66 us (3%)
  between operations  0.66 us (3%)
    pallas_call x1, Pallas kernels, local(): pl.pallas_call(functools.partial(seismogram_kernel, n, plane, cap, held,...  22.5 us
    unnamed x1, local copies, waits for them, and re-layouts  0.66 us

profile of v3, /device:TPU:11, one launch (start us, length us, event | category | flops | bytes accessed | tf_op | source)
XLA Modules:
  0.0 23.8 jit_solution(3165182068038384908)
XLA Ops:
  0.7 22.5 %seismograms.1 = f32[16,16,128]{2,1,0:T(8,128)S(1)} custom-call(s32[1]{0:T(128)S(6)} %copy.11.count_s, s32[1,32]{1,0:T(1,128)} %list_hbm.1, f32[1,6]{1,0:T(1,128)} %mech_hbm.1, bf16[16,4,6,16,128]{4,3,2,1,0:T(8,128)(2,1)} %bitcast.14, s32[16,128]{1,0:T(8,128)} %bitcast.15, f32[16,128]{1,0:T(8,128)} %bitcast.16, f32[16,128]{1,0:T(8,128)} %bitcast.17), custom_call_target="tpu_custom_call" | custom-call | tf_op jit(solution)/shard_map/seismograms/pallas_call | solution.py:359
  23.2 0.7 %copy.12 = f32[1,16,2,1024]{3,2,1,0:T(2,128)} copy(f32[1,16,2,1024]{3,2,1,0:T(2,128)S(1)} %bitcast.13) | data formatting | bytes 262144

commit v4 on v3

--- a/solution.py
+++ b/solution.py
@@ -27,6 +27,7 @@
     variations, rows = out_ref.shape[0], out_ref.shape[1]
     tiles = rows // comps
     half = rows // 2
+    chip = plane // 2
     mesh_id = pl.DeviceIdType.MESH
 
     barrier = pltpu.get_barrier_semaphore()
@@ -112,11 +113,9 @@
                                     device_id_type=mesh_id)
 
     def start_meta(there):
-        remote(table.at[there], want_v.at[me], send_m, recv_m.at[z], there).start()
-        remote(mech_row, gain_v.at[me], send_m, recv_m.at[z], there).start()
-
-    def wait_meta(q):
-        pltpu.make_async_copy(meta_bytes, meta_bytes, recv_m.at[q]).wait()
+        home = recv_m.at[2 * z + i_own // chip]
+        remote(table.at[there], want_v.at[me], send_m, home, there).start()
+        remote(mech_row, gain_v.at[me], send_m, home, there).start()
 
     def make_taps():
         i_row = lax.broadcasted_iota(jnp.int32, (LANES, LANES), 0)
@@ -226,29 +225,32 @@
         remote(outbox.at[there], inbox.at[me], send_t, recv_t.at[me // 2], there).start()
         remote(out_scale.at[there], in_scale.at[me], send_t, recv_t.at[me // 2], there).start()
 
-    chip = plane // 2
     steps = 4 * planes - 2
 
     def encode_step(u, carry):
         middle = u >= 6
-        k = jnp.where(middle, planes - 1 - (u - 6) // 4, jnp.where(u >= 4, 0, 1))
-        away = jnp.where(middle, (u - 6) % 4 >= 2, jnp.logical_or(u == 1, u == 2))
-        part = jnp.where(middle, (u - 6) % 2, jnp.logical_or(jnp.logical_or(u == 2, u == 3), u == 5).astype(jnp.int32))
+        w = (u - 6) // 2
+        k = jnp.where(middle, planes - 1 - w // 2, jnp.where(u >= 4, 0, 1))
+        away = jnp.where(middle, u % 2 == 1, jnp.logical_or(u == 1, u == 2))
+        second = jnp.logical_or(jnp.logical_or(u == 2, u == 3), u == 5).astype(jnp.int32)
+        part = jnp.where(middle, w % 2, second)
         q = z + jnp.where(away, -toward, toward) * k
+        side = (i_own // chip + part) % 2
 
         @pl.when(inside(q))
         def _():
-            @pl.when(jnp.logical_and(part == 0, k > 0))
+            @pl.when(k + part > 0)
             def _():
-                wait_meta(q)
-
-            @pl.when(jnp.logical_and(part == 0, k == 0))
-            def _():
-                beside_bytes = meta_bytes.at[pl.ds(0, (plane - 1) * (cap + 1))]
-                pltpu.make_async_copy(beside_bytes, beside_bytes, recv_m.at[z]).wait()
+                pltpu.make_async_copy(meta_bytes, meta_bytes, recv_m.at[2 * q + side]).wait()
+
+            if chip > 1:
+                @pl.when(k + part == 0)
+                def _():
+                    mates = meta_bytes.at[pl.ds(0, (chip - 1) * (cap + 1))]
+                    pltpu.make_async_copy(mates, mates, recv_m.at[2 * q + side]).wait()
 
             def one(t, carry):
-                there = q * plane + (i_own // chip * chip + part * chip + t) % plane
+                there = q * plane + side * chip + t
 
                 @pl.when(there != me)
                 def _():
@@ -265,11 +267,11 @@
 
     depth = tiles // 2
 
-    def add_traces(js):
+    def add_traces(js, groups):
         bases = [own_s[0, j * cap + slot] * points for j in js for slot in range(cap)]
         scales = [jnp.broadcast_to(in_scale[j][:, slot * (LANES // cap):slot * (LANES // cap) + 1], (8, LANES))
                   for j in js for slot in range(cap)]
-        for group in range(variations // 8):
+        for group in groups:
             part = slice(group * 8, group * 8 + 8)
             acc = [motion[comps + q, part, :] for q in range(rows)]
             for e, (base, scale) in enumerate(zip(bases, scales)):
@@ -297,26 +299,39 @@
             for q in range(rows):
                 motion[comps + q, part, :] = acc[q]
 
-    def arrive(t, carry):
+    def sources(t):
         ring = t // chip
         k = (ring + 1) // 2
         q = z + jnp.where(ring % 2 == 1, -toward, toward) * k
-        first = q * plane + ((i_own // 2 + t) % chip) * 2
+        return q, q * plane + ((i_own // 2 + t) % chip) * 2
+
+    def await_traces(first):
+        @pl.when(first == me // 2 * 2)
+        def _():
+            mate = trace_bytes.at[pl.ds(0, cap * points * half + 1)]
+            pltpu.make_async_copy(mate, mate, recv_t.at[first // 2]).wait()
+
+        @pl.when(first != me // 2 * 2)
+        def _():
+            pltpu.make_async_copy(trace_bytes, trace_bytes, recv_t.at[first // 2]).wait()
+
+    def arrive(t, carry):
+        q, first = sources(t)
 
         @pl.when(inside(q))
         def _():
-            @pl.when(first == me // 2 * 2)
-            def _():
-                mate = trace_bytes.at[pl.ds(0, cap * points * half + 1)]
-                pltpu.make_async_copy(mate, mate, recv_t.at[first // 2]).wait()
-
-            @pl.when(first != me // 2 * 2)
-            def _():
-                pltpu.make_async_copy(trace_bytes, trace_bytes, recv_t.at[first // 2]).wait()
-
-            add_traces([first, first + 1])
+            await_traces(first)
+            add_traces([first, first + 1], range(variations // 8))
 
         return carry
+
+    def convolve(v):
+        lhs = jnp.concatenate([motion[comps:comps + rows, v, :], motion[0:rows, v, :]], axis=1)
+        high = lhs.astype(jnp.bfloat16).astype(jnp.float32)
+        pair = jnp.concatenate([high, lhs - high], axis=0).astype(jnp.bfloat16)
+        main = jnp.dot(pair, high_taps[v], preferred_element_type=jnp.float32)
+        minor = jnp.dot(pair[:rows], low_taps[v], preferred_element_type=jnp.float32)
+        out_ref[v] = main[:rows] + (main[rows:] + minor)
 
     lax.fori_loop(0, 6, encode_step, 0)
     encode_own()
@@ -324,15 +339,14 @@
     early = jnp.where(inside(z + toward * (planes - 1)), chip, 0)
     lax.fori_loop(0, early, arrive, 0)
     lax.fori_loop(6, steps, encode_step, 0)
-    lax.fori_loop(early, (2 * planes - 1) * chip, arrive, 0)
-
-    for v in range(variations):
-        lhs = jnp.concatenate([motion[comps:comps + rows, v, :], motion[0:rows, v, :]], axis=1)
-        high = lhs.astype(jnp.bfloat16).astype(jnp.float32)
-        pair = jnp.concatenate([high, lhs - high], axis=0).astype(jnp.bfloat16)
-        main = jnp.dot(pair, high_taps[v], preferred_element_type=jnp.float32)
-        minor = jnp.dot(pair[:rows], low_taps[v], preferred_element_type=jnp.float32)
-        out_ref[v] = main[:rows] + (main[rows:] + minor)
+    last = 2 * jnp.where(toward > 0, planes - 1 - z, z) * chip + chip - 1
+    lax.fori_loop(early, last, arrive, 0)
+    _, first = sources(last)
+    await_traces(first)
+    for group in range(variations // 8):
+        add_traces([first, first + 1], [group])
+        for v in range(group * 8, group * 8 + 8):
+            convolve(v)
 
     others = pl.ds(0, n - 1)
     for box, sem in ((want_v, send_m), (gain_v, send_m), (outbox, send_t), (out_scale, send_t)):
@@ -384,9 +398,9 @@
             pltpu.VMEM(((listed + 1) * points, variations, LANES), jnp.int32),
             pltpu.VMEM(((listed + 1) * points, variations, LANES), jnp.int32),
             pltpu.VMEM(((listed + 1) * points, variations, LANES), jnp.float32),
-            pltpu.VMEM((plane * (cap + 1), 1, LANES), jnp.int32),
+            pltpu.VMEM((plane // 2 * (cap + 1), 1, LANES), jnp.int32),
             pltpu.VMEM((2 * (cap * points * rows // 2 + 1), 1, LANES), jnp.int32),
-            dma((7,)), pltpu.SemaphoreType.REGULAR((planes,)), dma, dma((planes,)), dma, dma((n // 2,)),
+            dma((7,)), pltpu.SemaphoreType.REGULAR((planes,)), dma, dma((2 * planes,)), dma, dma((n // 2,)),
         ],
         compiler_params=pltpu.CompilerParams(
             collective_id=0, has_side_effects=True, vmem_limit_bytes=32 << 20),

time: 24.1 us -> 23.5 us (0.975)
  Pallas kernels: 22.5 us -> 22 us
    pallas_call x1, Pallas kernels: 22.5 us -> 22 us  [local(): pl.pallas_call(functools.partial(seismogram_kernel, n, plane, cap, held,...]
where the time goes in v4:
time: 23.5 us; the launch traced here: 23.3 us
  Pallas kernels  22 us (94%)
  local copies, waits for them, and re-layouts  0.66 us (3%)
  between operations  0.66 us (3%)
    pallas_call x1, Pallas kernels, local(): pl.pallas_call(functools.partial(seismogram_kernel, n, plane, cap, held,...  22 us
    unnamed x1, local copies, waits for them, and re-layouts  0.66 us

profile of v4, /device:TPU:11, one launch (start us, length us, event | category | flops | bytes accessed | tf_op | source)
XLA Modules:
  0.0 23.3 jit_solution(4047977613316312886)
XLA Ops:
  0.7 22.0 %seismograms.1 = f32[16,16,128]{2,1,0:T(8,128)S(1)} custom-call(s32[1]{0:T(128)S(6)} %copy.11.count_s, s32[1,32]{1,0:T(1,128)} %list_hbm.1, f32[1,6]{1,0:T(1,128)} %mech_hbm.1, bf16[16,4,6,16,128]{4,3,2,1,0:T(8,128)(2,1)} %bitcast.14, s32[16,128]{1,0:T(8,128)} %bitcast.15, f32[16,128]{1,0:T(8,128)} %bitcast.16, f32[16,128]{1,0:T(8,128)} %bitcast.17), custom_call_target="tpu_custom_call" | custom-call | tf_op jit(solution)/shard_map/seismograms/pallas_call | solution.py:373
  22.7 0.7 %copy.12 = f32[1,16,2,1024]{3,2,1,0:T(2,128)} copy(f32[1,16,2,1024]{3,2,1,0:T(2,128)S(1)} %bitcast.13) | data formatting | bytes 262144

commit v5 on v4

--- a/solution.py
+++ b/solution.py
@@ -250,7 +250,7 @@
                     pltpu.make_async_copy(mates, mates, recv_m.at[2 * q + side]).wait()
 
             def one(t, carry):
-                there = q * plane + side * chip + t
+                there = q * plane + side * chip + jnp.where(k == 1, (t + i_own) % chip, t)
 
                 @pl.when(there != me)
                 def _():

time: 23.5 us -> 23.5 us (level)
  no operation moved by 1% of the time
where the time goes in v5:
time: 23.5 us; the launch traced here: 23.3 us
  Pallas kernels  22 us (94%)
  local copies, waits for them, and re-layouts  0.66 us (3%)
  between operations  0.66 us (3%)
    pallas_call x1, Pallas kernels, local(): pl.pallas_call(functools.partial(seismogram_kernel, n, plane, cap, held,...  22 us
    unnamed x1, local copies, waits for them, and re-layouts  0.66 us

profile of v5, /device:TPU:11, one launch (start us, length us, event | category | flops | bytes accessed | tf_op | source)
XLA Modules:
  0.0 23.3 jit_solution(2759586444926427464)
XLA Ops:
  0.7 22.0 %seismograms.1 = f32[16,16,128]{2,1,0:T(8,128)S(1)} custom-call(s32[1]{0:T(128)S(6)} %copy.11.count_s, s32[1,32]{1,0:T(1,128)} %list_hbm.1, f32[1,6]{1,0:T(1,128)} %mech_hbm.1, bf16[16,4,6,16,128]{4,3,2,1,0:T(8,128)(2,1)} %bitcast.14, s32[16,128]{1,0:T(8,128)} %bitcast.15, f32[16,128]{1,0:T(8,128)} %bitcast.16, f32[16,128]{1,0:T(8,128)} %bitcast.17), custom_call_target="tpu_custom_call" | custom-call | tf_op jit(solution)/shard_map/seismograms/pallas_call | solution.py:373
  22.7 0.7 %copy.12 = f32[1,16,2,1024]{3,2,1,0:T(2,128)} copy(f32[1,16,2,1024]{3,2,1,0:T(2,128)S(1)} %bitcast.13) | data formatting | bytes 262144

commit v6 on v5

--- a/solution.py
+++ b/solution.py
@@ -336,7 +336,7 @@
     lax.fori_loop(0, 6, encode_step, 0)
     encode_own()
     to_scalar.wait()
-    early = jnp.where(inside(z + toward * (planes - 1)), chip, 0)
+    early = jnp.where(inside(z + toward * (planes - 1)), chip if planes > 1 else 0, 0)
     lax.fori_loop(0, early, arrive, 0)
     lax.fori_loop(6, steps, encode_step, 0)
     last = 2 * jnp.where(toward > 0, planes - 1 - z, z) * chip + chip - 1

time: 23.5 us -> 23.5 us (level)
  no operation moved by 1% of the time
where the time goes in v6:
time: 23.5 us; the launch traced here: 23.3 us
  Pallas kernels  22 us (94%)
  local copies, waits for them, and re-layouts  0.66 us (3%)
  between operations  0.66 us (3%)
    pallas_call x1, Pallas kernels, local(): pl.pallas_call(functools.partial(seismogram_kernel, n, plane, cap, held,...  22 us
    unnamed x1, local copies, waits for them, and re-layouts  0.66 us

profile of v6, /device:TPU:11, one launch (start us, length us, event | category | flops | bytes accessed | tf_op | source)
XLA Modules:
  0.0 23.3 jit_solution(2759586444926427464)
XLA Ops:
  0.7 22.0 %seismograms.1 = f32[16,16,128]{2,1,0:T(8,128)S(1)} custom-call(s32[1]{0:T(128)S(6)} %copy.11.count_s, s32[1,32]{1,0:T(1,128)} %list_hbm.1, f32[1,6]{1,0:T(1,128)} %mech_hbm.1, bf16[16,4,6,16,128]{4,3,2,1,0:T(8,128)(2,1)} %bitcast.14, s32[16,128]{1,0:T(8,128)} %bitcast.15, f32[16,128]{1,0:T(8,128)} %bitcast.16, f32[16,128]{1,0:T(8,128)} %bitcast.17), custom_call_target="tpu_custom_call" | custom-call | tf_op jit(solution)/shard_map/seismograms/pallas_call | solution.py:373
  22.7 0.7 %copy.12 = f32[1,16,2,1024]{3,2,1,0:T(2,128)} copy(f32[1,16,2,1024]{3,2,1,0:T(2,128)S(1)} %bitcast.13) | data formatting | bytes 262144
